TPU v7x, 32 devices: a whole 2x2x4 slice. The times are simulated.
32 devices in a mesh: owner: 4 (over y, core), rows: 8 (over z, x).
Axes of the slice: x: 2, y: 2, z: 4, core: 2. Of those that a mesh axis runs over, the one named last changes fastest.
Arguments:
- train_gate: float32 [128, 2048, 768], P('owner', 'rows'), may hold values from -0.125 to 0.125
- train_up: float32 [128, 2048, 768], P('owner', 'rows'), may hold values from -0.125 to 0.125
- router_weight: float32 [2048, 128], P('rows', 'owner'), may hold values from -0.125 to 0.125
- router_gain: float32 [2048], P('rows'), may hold values from 0.25 to 1.75
Outputs:
- ready_gate: bfloat16 [128, 768, 2048], P(('owner', 'rows'))
- ready_up: bfloat16 [128, 768, 2048], P(('owner', 'rows'))
- serve_router: bfloat16 [2048, 128], replicated
All inputs are finite; a program needn't handle non-finite values.
Results may differ from a plain program's by a relative error of at most 0.001.
Values may be sent and summed in bfloat16 or wider, within the bound.
A program may use at most 192 MiB of HBM per device.

v0:
```python
import jax
import jax.numpy as jnp
from jax import lax
from jax.sharding import PartitionSpec as P


def on_device(train_gate, train_up, router_weight, router_gain):
    narrow_gate, narrow_up = (train_gate.astype(jnp.bfloat16), train_up.astype(jnp.bfloat16))
    ready_gate, ready_up = (
        lax.all_to_all(narrow_gate, "rows", split_axis=0, concat_axis=1, tiled=True),
        lax.all_to_all(narrow_up, "rows", split_axis=0, concat_axis=1, tiled=True),
    )
    ready_gate = jnp.transpose(ready_gate, (0, 2, 1))
    ready_up = jnp.transpose(ready_up, (0, 2, 1))
    part_router = (router_weight * router_gain[:, None]).astype(jnp.bfloat16)
    row_router = lax.all_gather(part_router, "rows", axis=0, tiled=True)
    serve_router = lax.all_gather(row_router, "owner", axis=1, tiled=True)
    return (ready_gate, ready_up, serve_router)


def solution(mesh):
    placed = (P("owner", "rows", None), P("owner", "rows", None), P("rows", "owner"), P("rows"))
    return jax.shard_map(
        on_device,
        mesh=mesh,
        in_specs=placed,
        out_specs=(P(("owner", "rows"), None, None), P(("owner", "rows"), None, None), P()),
        check_vma=False,
    )
```

profile of v0, /device:TPU:0, one launch (start us, length us, event | category | flops | bytes accessed | tf_op | source)
XLA Modules:
  0.0 672.7 jit_solution(13268045616997217038)
XLA Ops:
  0.6 13.2 %convert_element_type.9 = bf16[32,256,768]{2,1,0:T(8,128)(2,1)} convert(f32[32,256,768]{2,1,0:T(8,128)} %param.4) | non-fusion elementwise | flops 6291456 | bytes 37748736 | tf_op jit(solution)/shard_map/convert_element_type | solution.py:8
  13.8 7.3 %all-to-all-start = ((bf16[32,256,768]{2,1,0:T(8,128)(2,1)}), bf16[32,256,768]{2,1,0:T(8,128)(2,1)}, u32[]{:S(2)}, u32[]{:S(2)}) async-start(bf16[32,256,768]{2,1,0:T(8,128)(2,1)} %convert_element_type.9), calls=%async_computation | async-start | bytes 25165824 | tf_op jit(solution)/shard_map/all_to_all | solution.py:10
  21.1 13.4 %convert_element_type.10 = bf16[32,256,768]{2,1,0:T(8,128)(2,1)} convert(f32[32,256,768]{2,1,0:T(8,128)} %param.5) | non-fusion elementwise | flops 6291456 | bytes 37748736 | tf_op jit(solution)/shard_map/convert_element_type | solution.py:8
  34.5 0.0 copy-start
  34.5 0.0 copy-start.1
  34.5 259.7 %all-to-all-done = bf16[32,256,768]{2,1,0:T(8,128)(2,1)} async-done(((bf16[32,256,768]{2,1,0:T(8,128)(2,1)}), bf16[32,256,768]{2,1,0:T(8,128)(2,1)}, u32[]{:S(2)}, u32[]{:S(2)}) %all-to-all-start) | async-done | bytes 12582944 | tf_op jit(solution)/shard_map/all_to_all | solution.py:10
  294.2 5.3 all-to-all-start.1
  299.5 0.0 copy-done
  299.5 0.0 copy-done.1
  299.5 292.2 %all_gather.6 = bf16[2048,32]{0,1:T(8,128)(2,1)S(1)} all-gather(bf16[256,32]{0,1:T(8,128)(2,1)S(1)} %multiply_convert_fusion), channel_id=1, replica_groups=mesh['owner'=4,'rows'=8] {'rows'}, dimensions={0}, use_global_device_ids=true | all-gather | bytes 147456 | tf_op jit(solution)/shard_map/all_gather | solution.py:16
  591.8 7.2 %all_gather.7 = bf16[2048,128]{0,1:T(8,128)(2,1)S(1)} all-gather(bf16[2048,32]{0,1:T(8,128)(2,1)S(1)} %all_gather.6), channel_id=1, replica_groups=mesh['owner'=4,'rows'=8] {'owner'}, dimensions={1}, use_global_device_ids=true | all-gather | bytes 655360 | tf_op jit(solution)/shard_map/all_gather | solution.py:17
  598.9 1.0 copy.12
  599.9 16.9 %copy.10 = bf16[8,4,256,768]{2,0,3,1:T(8,128)(2,1)} copy(bf16[8,4,256,768]{3,2,1,0:T(8,128)(2,1)} %bitcast) | data formatting | bytes 25165824 | tf_op jit(solution)/shard_map/all_to_all | solution.py:10
  616.8 19.5 %all_to_all.29 = bf16[4,2048,768]{1,2,0:T(8,128)(2,1)} reshape(bf16[4,8,256,768]{2,1,3,0:T(8,128)(2,1)} %bitcast.14) | data formatting | bytes 25165824 | tf_op jit(solution)/shard_map/all_to_all | solution.py:10
  636.3 0.0 all-to-all-done.1
  636.3 16.9 %copy.11 = bf16[8,4,256,768]{2,0,3,1:T(8,128)(2,1)} copy(bf16[8,4,256,768]{3,2,1,0:T(8,128)(2,1)} %bitcast.3) | data formatting | bytes 25165824 | tf_op jit(solution)/shard_map/all_to_all | solution.py:11
  653.2 19.5 %all_to_all.33 = bf16[4,2048,768]{1,2,0:T(8,128)(2,1)} reshape(bf16[4,8,256,768]{2,1,3,0:T(8,128)(2,1)} %bitcast.15) | data formatting | bytes 25165824 | tf_op jit(solution)/shard_map/all_to_all | solution.py:11
  (1 shorter events, 0.0 us)
Async XLA Ops:
  13.8 280.3 %all-to-all-start = ((bf16[32,256,768]{2,1,0:T(8,128)(2,1)}), bf16[32,256,768]{2,1,0:T(8,128)(2,1)}, u32[]{:S(2)}, u32[]{:S(2)}) async-start(bf16[32,256,768]{2,1,0:T(8,128)(2,1)} %convert_element_type.9), calls=%async_computation | async-start | bytes 25165824 | tf_op jit(solution)/shard_map/all_to_all | solution.py:10
  34.5 265.0 %copy-start = (f32[256,32]{0,1:T(8,128)S(1)}, f32[256,32]{0,1:T(8,128)}, u32[]{:S(2)}) copy-start(f32[256,32]{0,1:T(8,128)} %param.6) | copy-start | bytes 98308
  34.5 265.0 %copy-start.1 = (f32[256]{0:T(256)S(1)}, f32[256]{0:T(256)}, u32[]{:S(2)}) copy-start(f32[256]{0:T(256)} %param.7) | copy-start | bytes 3076
  294.2 342.1 %all-to-all-start.1 = ((bf16[32,256,768]{2,1,0:T(8,128)(2,1)}), bf16[32,256,768]{2,1,0:T(8,128)(2,1)}, u32[]{:S(2)}, u32[]{:S(2)}) async-start(bf16[32,256,768]{2,1,0:T(8,128)(2,1)} %convert_element_type.10), calls=%async_computation.1 | async-start | bytes 25165824 | tf_op jit(solution)/shard_map/all_to_all | solution.py:11
where the time goes:
time: 675 us; the launch traced here: 673 us
  blocking collectives  299 us (44%)
  waiting for transfers between devices  260 us (39%)
  local copies, waits for them, and re-layouts  73.7 us (11%)
  other arithmetic  26.6 us (4%)
  starting transfers between devices  12.6 us (2%)
    all_gather x1, blocking collectives, on_device(): row_router = lax.all_gather(part_router, 'rows', axis=0, tiled=True)  292 us
    all_to_all x1, waiting for transfers between devices, on_device(): lax.all_to_all(narrow_gate, 'rows', split_axis=0, concat_axis=1, tiled=True)  260 us
    all_to_all x2, local copies, waits for them, and re-layouts, on_device(): lax.all_to_all(narrow_up, 'rows', split_axis=0, concat_axis=1, tiled=True)  36.4 us
    all_to_all x2, local copies, waits for them, and re-layouts, on_device(): lax.all_to_all(narrow_gate, 'rows', split_axis=0, concat_axis=1, tiled=True)  36.3 us
  transfers between devices with their start and end apart: 2, of which 1 were waited for; matrix products, arithmetic and copies ran while one was open for 5% of the time, Pallas kernels for 0%

commit v1 on v0

--- a/solution.py
+++ b/solution.py
@@ -2,6 +2,12 @@
 import jax.numpy as jnp
 from jax import lax
 from jax.sharding import PartitionSpec as P
+
+
+def all_parts(x, name, dim):
+    terms = lax.all_gather(x, name, axis=0, tiled=False)
+    whole = jnp.concatenate(terms, axis=dim)
+    return whole
 
 
 def on_device(train_gate, train_up, router_weight, router_gain):
@@ -14,7 +20,7 @@
     ready_up = jnp.transpose(ready_up, (0, 2, 1))
     part_router = (router_weight * router_gain[:, None]).astype(jnp.bfloat16)
     row_router = lax.all_gather(part_router, "rows", axis=0, tiled=True)
-    serve_router = lax.all_gather(row_router, "owner", axis=1, tiled=True)
+    serve_router = all_parts(row_router, "owner", 1)
     return (ready_gate, ready_up, serve_router)
 
 

time: 675 us -> 675 us (level)
  no operation moved by 1% of the time
where the time goes in v1:
time: 675 us; the launch traced here: 673 us
  blocking collectives  299 us (44%)
  waiting for transfers between devices  260 us (39%)
  local copies, waits for them, and re-layouts  74.4 us (11%)
  other arithmetic  26.6 us (4%)
  starting transfers between devices  12.6 us (2%)
    all_gather x1, blocking collectives, on_device(): row_router = lax.all_gather(part_router, 'rows', axis=0, tiled=True)  292 us
    all_to_all x1, waiting for transfers between devices, on_device(): lax.all_to_all(narrow_gate, 'rows', split_axis=0, concat_axis=1, tiled=True)  260 us
    all_to_all x2, local copies, waits for them, and re-layouts, on_device(): lax.all_to_all(narrow_up, 'rows', split_axis=0, concat_axis=1, tiled=True)  36.4 us
    all_to_all x2, local copies, waits for them, and re-layouts, on_device(): lax.all_to_all(narrow_gate, 'rows', split_axis=0, concat_axis=1, tiled=True)  36.3 us
  transfers between devices with their start and end apart: 2, of which 1 were waited for; matrix products, arithmetic and copies ran while one was open for 5% of the time, Pallas kernels for 0%

profile of v1, /device:TPU:0, one launch (start us, length us, event | category | flops | bytes accessed | tf_op | source)
XLA Modules:
  0.0 673.3 jit_solution(9759219024306133304)
XLA Ops:
  0.6 13.2 %convert_element_type.9 = bf16[32,256,768]{2,1,0:T(8,128)(2,1)} convert(f32[32,256,768]{2,1,0:T(8,128)} %param.4) | non-fusion elementwise | flops 6291456 | bytes 37748736 | tf_op jit(solution)/shard_map/convert_element_type | solution.py:14
  13.8 7.3 %all-to-all-start = ((bf16[32,256,768]{2,1,0:T(8,128)(2,1)}), bf16[32,256,768]{2,1,0:T(8,128)(2,1)}, u32[]{:S(2)}, u32[]{:S(2)}) async-start(bf16[32,256,768]{2,1,0:T(8,128)(2,1)} %convert_element_type.9), calls=%async_computation | async-start | bytes 25165824 | tf_op jit(solution)/shard_map/all_to_all | solution.py:16
  21.1 13.4 %convert_element_type.10 = bf16[32,256,768]{2,1,0:T(8,128)(2,1)} convert(f32[32,256,768]{2,1,0:T(8,128)} %param.5) | non-fusion elementwise | flops 6291456 | bytes 37748736 | tf_op jit(solution)/shard_map/convert_element_type | solution.py:14
  34.5 0.0 copy-start
  34.5 0.0 copy-start.1
  34.5 259.7 %all-to-all-done = bf16[32,256,768]{2,1,0:T(8,128)(2,1)} async-done(((bf16[32,256,768]{2,1,0:T(8,128)(2,1)}), bf16[32,256,768]{2,1,0:T(8,128)(2,1)}, u32[]{:S(2)}, u32[]{:S(2)}) %all-to-all-start) | async-done | bytes 12582944 | tf_op jit(solution)/shard_map/all_to_all | solution.py:16
  294.2 5.3 all-to-all-start.1
  299.5 0.0 copy-done
  299.5 0.0 copy-done.1
  299.5 292.2 %all_gather.9 = bf16[2048,32]{0,1:T(8,128)(2,1)S(1)} all-gather(bf16[256,32]{0,1:T(8,128)(2,1)S(1)} %multiply_convert_fusion), channel_id=1, replica_groups=mesh['owner'=4,'rows'=8] {'rows'}, dimensions={0}, use_global_device_ids=true | all-gather | bytes 147456 | tf_op jit(solution)/shard_map/all_gather | solution.py:22
  591.8 7.2 %all-gather = bf16[8192,32]{0,1:T(8,128)(2,1)S(1)} all-gather(bf16[2048,32]{0,1:T(8,128)(2,1)S(1)} %all_gather.9), channel_id=2, replica_groups=mesh['owner'=4,'rows'=8] {'owner'}, dimensions={0}, use_global_device_ids=true | all-gather | bytes 655360 | tf_op jit(solution)/shard_map/all_gather | solution.py:8
  598.9 0.4 reshape.15
  599.3 0.3 copy.15
  599.6 1.0 copy.16
  600.6 16.9 %copy.13 = bf16[8,4,256,768]{2,0,3,1:T(8,128)(2,1)} copy(bf16[8,4,256,768]{3,2,1,0:T(8,128)(2,1)} %bitcast) | data formatting | bytes 25165824 | tf_op jit(solution)/shard_map/all_to_all | solution.py:16
  617.5 19.5 %all_to_all.29 = bf16[4,2048,768]{1,2,0:T(8,128)(2,1)} reshape(bf16[4,8,256,768]{2,1,3,0:T(8,128)(2,1)} %bitcast.18) | data formatting | bytes 25165824 | tf_op jit(solution)/shard_map/all_to_all | solution.py:16
  637.0 0.0 all-to-all-done.1
  637.0 16.9 %copy.14 = bf16[8,4,256,768]{2,0,3,1:T(8,128)(2,1)} copy(bf16[8,4,256,768]{3,2,1,0:T(8,128)(2,1)} %bitcast.3) | data formatting | bytes 25165824 | tf_op jit(solution)/shard_map/all_to_all | solution.py:17
  653.9 19.5 %all_to_all.33 = bf16[4,2048,768]{1,2,0:T(8,128)(2,1)} reshape(bf16[4,8,256,768]{2,1,3,0:T(8,128)(2,1)} %bitcast.19) | data formatting | bytes 25165824 | tf_op jit(solution)/shard_map/all_to_all | solution.py:17
  (1 shorter events, 0.0 us)
Async XLA Ops:
  13.8 280.3 %all-to-all-start = ((bf16[32,256,768]{2,1,0:T(8,128)(2,1)}), bf16[32,256,768]{2,1,0:T(8,128)(2,1)}, u32[]{:S(2)}, u32[]{:S(2)}) async-start(bf16[32,256,768]{2,1,0:T(8,128)(2,1)} %convert_element_type.9), calls=%async_computation | async-start | bytes 25165824 | tf_op jit(solution)/shard_map/all_to_all | solution.py:16
  34.5 265.0 %copy-start = (f32[256,32]{0,1:T(8,128)S(1)}, f32[256,32]{0,1:T(8,128)}, u32[]{:S(2)}) copy-start(f32[256,32]{0,1:T(8,128)} %param.6) | copy-start | bytes 98308
  34.5 265.0 %copy-start.1 = (f32[256]{0:T(256)S(1)}, f32[256]{0:T(256)}, u32[]{:S(2)}) copy-start(f32[256]{0:T(256)} %param.7) | copy-start | bytes 3076
  294.2 342.8 %all-to-all-start.1 = ((bf16[32,256,768]{2,1,0:T(8,128)(2,1)}), bf16[32,256,768]{2,1,0:T(8,128)(2,1)}, u32[]{:S(2)}, u32[]{:S(2)}) async-start(bf16[32,256,768]{2,1,0:T(8,128)(2,1)} %convert_element_type.10), calls=%async_computation.1 | async-start | bytes 25165824 | tf_op jit(solution)/shard_map/all_to_all | solution.py:17
